TPU v7x, 32 devices: a whole 2x2x4 slice. The times are simulated.
32 devices in a mesh: dp: 8 (over y, x, core), tensor: 4 (over z).
Axes of the slice: x: 2, y: 2, z: 4, core: 2. Of those that a mesh axis runs over, the one named last changes fastest.
Arguments:
- acts: bfloat16 [1024, 4096], P('dp'), may hold values from -6 to 6
- grad_out: bfloat16 [1024, 14336], P('dp', 'tensor'), may hold values from -0.1875 to 0.1875
- selected: int32 [4, 4], P('tensor'), may hold values from 0 to 27, as said below
- owner: int32 [4, 192, 1], P('tensor'), may hold values from 0 to 7; in each aligned block of 192 rows (0 to 191, 192 to 383, ..., all dimensions but the last counted through in order) at most 36 rows name the same one
- sel_weight: float32 [4096, 2048], P('dp', 'tensor'), may hold values from -3 to 3
- sel_moment: float32 [4096, 2048], P('dp', 'tensor'), may hold values from -3 to 3
- sel_second: float32 [4096, 2048], P('dp', 'tensor'), may hold values from 0.01 to 1
- off_weight: float32 [8, 4, 36, 512, 128], P('dp', 'tensor'), may hold values from -3 to 3
- off_moment: float32 [8, 4, 36, 512, 128], P('dp', 'tensor'), may hold values from -3 to 3
- off_second: float32 [8, 4, 36, 512, 128], P('dp', 'tensor'), may hold values from 0.01 to 1
Outputs:
- column_norm: float32 [14336], P('tensor')
- sel_weight_new: float32 [4096, 2048], P('dp', 'tensor')
- sel_moment_new: float32 [4096, 2048], P('dp', 'tensor')
- sel_second_new: float32 [4096, 2048], P('dp', 'tensor')
- off_weight_new: float32 [8, 4, 36, 512, 128], P('dp', 'tensor')
- off_moment_new: float32 [8, 4, 36, 512, 128], P('dp', 'tensor')
- off_second_new: float32 [8, 4, 36, 512, 128], P('dp', 'tensor')
Inputs may be any that keep to these rules, and one draw needn't show every extreme that they name: `selected`: each row names 4 tile. For each index of tensor, no owner receives more than 36 pieces, and some owner receives exactly 36.
All inputs are finite; a program needn't handle non-finite values.
Results may differ from a plain program's by a relative error of at most 0.0017.
Values may be sent and summed in bfloat16 or wider, within the bound.
A program may use at most 192 MiB of HBM per device.

v0:
```python
import jax
import jax.numpy as jnp
from jax import lax
from jax.sharding import PartitionSpec as P

TILE = 128


beta_one = 0.9
beta_two = 0.95
adam_eps = 1e-08
learn_rate = 0.01
decay_rate = 0.1
step_count = 10.0


def adam_update(weight, moment, second, grad):
    moment_new = beta_one * moment + (1.0 - beta_one) * grad
    second_new = beta_two * second + (1.0 - beta_two) * grad * grad
    first_fix = 1.0 - beta_one**step_count
    second_fix = 1.0 - beta_two**step_count
    update = moment_new / first_fix / (jnp.sqrt(second_new / second_fix) + adam_eps)
    return (weight - learn_rate * (update + decay_rate * weight), moment_new, second_new)


def rest_tiles(selected_row, tiles_here):
    tiles = jnp.arange(tiles_here, dtype=jnp.int32)
    chosen = jnp.any(tiles[:, None] == selected_row[None, :], axis=1).astype(jnp.int32)
    order = jnp.argsort(chosen * tiles_here + tiles)
    return order[: tiles_here - selected_row.shape[0]]


def slot_numbers(owner_row):
    places = jnp.arange(owner_row.shape[0], dtype=jnp.int32)
    earlier = (owner_row[:, None] == owner_row[None, :]) & (places[:, None] > places[None, :])
    return jnp.sum(earlier.astype(jnp.int32), axis=1)


def contract_tokens(left, right):
    return lax.dot_general(
        left, right, (((0,), (0,)), ((), ())), preferred_element_type=jnp.float32
    )


def body(
    acts,
    grad_out,
    selected,
    owner,
    sel_weight,
    sel_moment,
    sel_second,
    off_weight,
    off_moment,
    off_second,
):
    group_size = lax.axis_size("dp")
    tokens_here, rows_all = acts.shape
    cols_here = grad_out.shape[1]
    tiles_here = cols_here // TILE
    sel_count = selected.shape[1]
    rest_count = tiles_here - sel_count
    row_block = rows_all // group_size
    capacity = off_weight.shape[2]
    piece_count = rest_count * group_size
    selected_row = selected[0]
    owner_row = owner[0, :, 0]
    rest_row = rest_tiles(selected_row, tiles_here)
    grad_tiles = grad_out.reshape(tokens_here, tiles_here, TILE)
    zero_half = jnp.zeros((), jnp.bfloat16)
    gram = lax.dot_general(acts, acts, (((1,), (1,)), ((), ())), preferred_element_type=jnp.float32)
    grad_wide = grad_out.astype(jnp.float32)
    squares = jnp.sum(grad_wide * jnp.dot(gram, grad_wide, precision=lax.Precision.HIGHEST), axis=0)
    column_norm = jnp.sqrt(lax.psum(squares, "dp"))
    sel_grad = jnp.take(grad_tiles, selected_row, axis=1).reshape(tokens_here, sel_count * TILE)
    sel_sum = lax.psum_scatter(
        contract_tokens(acts, sel_grad), "dp", scatter_dimension=0, tiled=True
    )
    new_sel = adam_update(sel_weight, sel_moment, sel_second, sel_sum)
    rest_grad = jnp.moveaxis(jnp.take(grad_tiles, rest_row, axis=1), 1, 0)

    def tile_partial(column):
        return contract_tokens(acts, column).astype(jnp.bfloat16)

    partials = lax.map(tile_partial, rest_grad).reshape(rest_count, group_size, row_block, TILE)
    slot_index = slot_numbers(owner_row)
    target = owner_row * capacity + slot_index
    source = (
        jnp.full((group_size * capacity,), piece_count, jnp.int32)
        .at[target]
        .set(jnp.arange(piece_count, dtype=jnp.int32))
    )
    filled = source < piece_count
    flat_pieces = partials.reshape(piece_count, row_block, TILE)
    outgoing = jnp.where(
        filled[:, None, None], flat_pieces[jnp.minimum(source, piece_count - 1)], zero_half
    )
    received = lax.all_to_all(
        outgoing.reshape(group_size, capacity, row_block, TILE),
        "dp",
        split_axis=0,
        concat_axis=0,
        tiled=True,
    )
    offload = jnp.sum(received, axis=0, dtype=jnp.float32).astype(jnp.bfloat16)
    off_grad = offload.astype(jnp.float32).reshape(off_weight.shape)
    new_off = adam_update(off_weight, off_moment, off_second, off_grad)
    return (column_norm, new_sel[0], new_sel[1], new_sel[2], new_off[0], new_off[1], new_off[2])


def solution(mesh):
    placed = (
        P("dp", None),
        P("dp", "tensor"),
        P("tensor", None),
        P("tensor", None, None),
        P("dp", "tensor"),
        P("dp", "tensor"),
        P("dp", "tensor"),
        P("dp", "tensor", None, None, None),
        P("dp", "tensor", None, None, None),
        P("dp", "tensor", None, None, None),
    )
    return jax.shard_map(
        body,
        mesh=mesh,
        in_specs=placed,
        out_specs=(
            P("tensor"),
            P("dp", "tensor"),
            P("dp", "tensor"),
            P("dp", "tensor"),
            P("dp", "tensor", None, None, None),
            P("dp", "tensor", None, None, None),
            P("dp", "tensor", None, None, None),
        ),
        check_vma=False,
    )
```

profile of v0, /device:TPU:0, one launch (start us, length us, event | category | flops | bytes accessed | tf_op | source)
XLA Modules:
  0.0 670.7 jit_solution(16563332979148506943)
XLA Ops:
  8.8 1.2 scatter_custom_fusion
  10.0 1.6 copy.48
  13.0 1.6 sort.17
  16.4 82.4 %while.10 = (s32[]{:T(128)}, bf16[24,4096,128]{2,1,0:T(8,128)(2,1)}, bf16[24,128,128]{2,1,0:T(8,128)(2,1)}, bf16[128,4096]{1,0:T(8,128)(2,1)}, s32[]{:T(128)}) while((s32[]{:T(128)}, bf16[24,4096,128]{2,1,0:T(8,128)(2,1)}, bf16[24,128,128]{2,1,0:T(8,128)(2,1)}, bf16[128,4096]{1,0:T(8,128)(2,1)}, s32[]{:T(128)}) %tuple.31), condition=%wide.region_8.9_spmd, body=%wide.region_7.8_spmd.sunk | while | flops 134742016 | bytes 6325309 | solution.py:85
  16.4 1.7 fusion.29
  18.7 1.0 constant_dynamic-update-slice_fusion.2
  19.8 1.7 fusion.29
  23.2 1.7 fusion.29
  25.5 1.1 constant_dynamic-update-slice_fusion.2
  26.6 1.7 fusion.29
  29.0 1.1 constant_dynamic-update-slice_fusion.2
  30.0 1.7 fusion.29
  32.4 1.1 constant_dynamic-update-slice_fusion.2
  33.5 1.7 fusion.29
  35.8 1.1 constant_dynamic-update-slice_fusion.2
  36.9 1.7 fusion.29
  39.3 1.1 constant_dynamic-update-slice_fusion.2
  40.4 1.7 fusion.29
  43.8 1.7 fusion.29
  46.2 1.1 constant_dynamic-update-slice_fusion.2
  47.2 1.7 fusion.29
  49.6 1.1 constant_dynamic-update-slice_fusion.2
  50.7 1.7 fusion.29
  53.1 1.1 constant_dynamic-update-slice_fusion.2
  54.1 1.7 fusion.29
  56.5 1.1 constant_dynamic-update-slice_fusion.2
  57.6 1.7 fusion.29
  59.9 1.1 constant_dynamic-update-slice_fusion.2
  61.0 1.7 fusion.29
  63.4 1.1 constant_dynamic-update-slice_fusion.2
  64.4 1.7 fusion.29
  66.8 1.1 constant_dynamic-update-slice_fusion.2
  67.9 1.7 fusion.29
  70.2 1.1 constant_dynamic-update-slice_fusion.2
  71.3 1.7 fusion.29
  73.7 1.0 constant_dynamic-update-slice_fusion.2
  74.7 1.7 fusion.29
  78.1 1.7 fusion.29
  80.5 1.1 constant_dynamic-update-slice_fusion.2
  81.6 1.7 fusion.29
  84.0 1.1 constant_dynamic-update-slice_fusion.2
  85.0 1.7 fusion.29
  87.4 1.1 constant_dynamic-update-slice_fusion.2
  88.4 1.7 fusion.29
  90.8 1.1 constant_dynamic-update-slice_fusion.2
  91.9 1.7 fusion.29
  94.3 1.1 constant_dynamic-update-slice_fusion.2
  95.4 1.7 fusion.29
  97.7 1.0 constant_dynamic-update-slice_fusion.2
  98.9 23.4 %gather_fusion.2 = bf16[288,512,128]{2,1,0:T(8,128)(2,1)} fusion(bf16[192,512,128]{2,1,0:T(8,128)(2,1)} %bitcast.50, s32[1024]{0:T(1024)S(1)} %pad_clamp_fusion), kind=kCustom, calls=%fused_computation.2 | custom fusion | bytes 75498624 | tf_op jit(solution)/shard_map/gather | solution.py:96
  122.3 25.6 %broadcast_select_fusion = bf16[8,36,512,128]{3,2,1,0:T(8,128)(2,1)} fusion(bf16[8,36,512,128]{3,2,1,0:T(8,128)(2,1)} %bitcast.49, pred[8,36]{1,0:T(8,128)(4,1)S(1)} %broadcast_in_dim.59), kind=kLoop, calls=%fused_computation.10 | loop fusion | flops 18874368 | bytes 75497760 | tf_op jit(solution)/shard_map/jit(_where)/select_n | solution.py:95
  147.9 7.6 %all-to-all-start = ((bf16[8,36,512,128]{3,2,1,0:T(8,128)(2,1)}), bf16[8,36,512,128]{3,2,1,0:T(8,128)(2,1)}, u32[]{:S(2)}, u32[]{:S(2)}) async-start(bf16[8,36,512,128]{3,2,1,0:T(8,128)(2,1)} %broadcast_select_fusion), calls=%async_computation.1 | async-start | bytes 75497472 | tf_op jit(solution)/shard_map/all_to_all | solution.py:98
  156.5 4.6 convolution_bitcast_fusion
  161.2 1.6 copy.47
  162.8 1.6 copy.51
  164.3 2.5 copy.53
  167.3 2.5 fusion.6
  169.8 445.0 %psum.7 = f32[3584]{0:T(1024)S(1)} all-reduce(f32[3584]{0:T(1024)S(1)} %fusion.6), channel_id=1, replica_groups=mesh['dp'=8,'tensor'=4] {'dp'}, use_global_device_ids=true, to_apply=%region_1.0 | all-reduce | flops 3584 | bytes 28672 | tf_op jit(solution)/shard_map/psum | solution.py:74
  615.5 3.6 multiply_subtract_fusion.1
  619.1 2.5 copy.56
  621.7 2.5 copy.57
  624.2 1.3 copy.58
  625.5 15.6 %reduce_sum.35 = bf16[36,512,128]{2,1,0:T(8,128)(2,1)} reduce(bf16[8,36,512,128]{3,2,1,0:T(8,128)(2,1)} %all-to-all-done, bf16[]{:T(256)} %constant.45.clone.1), dimensions={0}, to_apply=%region_9.10 | reduce | flops 16515072 | bytes 42467328 | tf_op jit(solution)/shard_map/reduce_sum | solution.py:105
  641.1 22.8 %multiply_subtract_fusion = (f32[1,1,36,512,128]{4,3,2,1,0:T(8,128)}, f32[1,1,36,512,128]{4,3,2,1,0:T(8,128)}, f32[1,1,36,512,128]{4,3,2,1,0:T(8,128)}) fusion(f32[1,1,36,512,128]{4,3,2,1,0:T(8,128)} %param.19, bf16[36,512,128]{2,1,0:T(8,128)(2,1)} %reduce_sum.35, f32[1,1,36,512,128]{4,3,2,1,0:T(8,128)} %param.20, f32[1,1,36,512,128]{4,3,2,1,0:T(8,128)} %param.21), kind=kLoop, calls=%fused_computation.16 | loop fusion | flops 37748736 | bytes 61341696 | tf_op jit(solution)/shard_map/sub | solution.py:23
  (60 shorter events, 25.9 us)
Async XLA Ops:
  147.9 7.7 %copy-start.1 = (s32[1,4]{1,0:T(1,128)S(1)}, s32[1,4]{1,0:T(1,128)}, u32[]{:S(2)}) copy-start(s32[1,4]{1,0:T(1,128)} %param.14) | copy-start | bytes 52
  147.9 8.6 %copy-start = (bf16[128,4096]{1,0:T(8,128)(2,1)S(1)}, bf16[128,4096]{1,0:T(8,128)(2,1)}, u32[]{:S(2)}) copy-start(bf16[128,4096]{1,0:T(8,128)(2,1)} %get-tuple-element.119) | copy-start | bytes 3145732
  147.9 477.6 %all-to-all-start = ((bf16[8,36,512,128]{3,2,1,0:T(8,128)(2,1)}), bf16[8,36,512,128]{3,2,1,0:T(8,128)(2,1)}, u32[]{:S(2)}, u32[]{:S(2)}) async-start(bf16[8,36,512,128]{3,2,1,0:T(8,128)(2,1)} %broadcast_select_fusion), calls=%async_computation.1 | async-start | bytes 75497472 | tf_op jit(solution)/shard_map/all_to_all | solution.py:98
  155.5 460.0 %reduce-scatter.2.cloned.1.call-start = ((), (), s32[]{:S(2)}) async-start(), calls=%async_computation.2 | async-start | bytes 9437184 | tf_op jit(solution)/shard_map/reduce_scatter | solution.py:76
Sparse Core Ops, SparseCore 0:
  161.3 247.7 reduce-scatter.1
where the time goes:
time: 672 us; the launch traced here: 671 us
  blocking collectives  445 us (66%)
  local copies, waits for them, and re-layouts  82.4 us (12%)
  other arithmetic  72.8 us (11%)
  matrix products  48.3 us (7%)
  between operations  14.2 us (2%)
  starting transfers between devices  7.63 us (1%)
    psum x1, blocking collectives, body(): column_norm = jnp.sqrt(lax.psum(squares, 'dp'))  445 us
    dot_general x25, matrix products, contract_tokens(): lax.dot_general(left, right, (((0,), (0,)), ((), ())), preferred_element_...  45.4 us
    dynamic_update_slice x48, local copies, waits for them, and re-layouts, body(): lax.map(tile_partial, rest_grad)  41.3 us
    sub x2, other arithmetic, adam_update(): weight - learn_rate * (update + decay_rate * weight)  26.4 us
    select_n x1, other arithmetic, body(): jnp.where(filled[:, None, None], flat_pieces[jnp.minimum(source, piece_co...  25.6 us
    gather x1, local copies, waits for them, and re-layouts, body(): flat_pieces[jnp.minimum(source, piece_count - 1)]  23.4 us
    reduce_sum x1, other arithmetic, body(): offload = jnp.sum(received, axis=0, dtype=jnp.float32).astype(jnp.bfloat16)  15.6 us
    unnamed x11, local copies, waits for them, and re-layouts  13.6 us
  transfers between devices with their start and end apart: 2, of which 0 were waited for; matrix products, arithmetic and copies ran while one was open for 4% of the time, Pallas kernels for 0%

commit v1 on v0

v1 whole, which is shorter than its diff:
```python
import functools

import jax
import jax.numpy as jnp
from jax import lax
from jax.experimental import pallas as pl
from jax.experimental.pallas import tpu as pltpu
from jax.sharding import PartitionSpec as P

TILE = 128
VMEM_LIMIT = 56 * 1024 * 1024


beta_one = 0.9
beta_two = 0.95
adam_eps = 1e-08
learn_rate = 0.01
decay_rate = 0.1
step_count = 10.0


def adam_update(weight, moment, second, grad):
    moment_new = beta_one * moment + (1.0 - beta_one) * grad
    second_new = beta_two * second + (1.0 - beta_two) * grad * grad
    first_fix = 1.0 - beta_one**step_count
    second_fix = 1.0 - beta_two**step_count
    update = moment_new / first_fix / (jnp.sqrt(second_new / second_fix) + adam_eps)
    return (weight - learn_rate * (update + decay_rate * weight), moment_new, second_new)


MESH = pl.DeviceIdType.MESH


def flip_bits(index, mask):
    result, bit = index, 1
    while bit <= mask:
        if mask & bit:
            result = result + bit * (1 - 2 * ((index // bit) % 2))
        bit *= 2
    return result


def gather_kernel(
    n,
    tile_slot,
    block_slot,
    sel_tile,
    acts,
    acts_t,
    grad,
    offload,
    sel_sum,
    norm,
    total,
    squares,
    send_sem,
    recv_a,
    recv_g,
    send_q,
    recv_q,
    *held,
):
    held_a, held_g = (acts_t,) + held[: n - 1], (grad,) + held[n - 1 :]
    me = lax.axis_index("dp")
    capacity = offload.shape[0]
    sel_count = sel_tile.shape[0]
    rows_all = acts.shape[1]

    barrier = pltpu.get_barrier_semaphore()
    for mask in range(1, n):
        pl.semaphore_signal(
            barrier, inc=1, device_id={"dp": flip_bits(me, mask)}, device_id_type=MESH
        )
    pl.semaphore_wait(barrier, n - 1)

    started = []

    def block_of(kind, mask):
        return (held_a if kind == "a" else held_g)[mask]

    def copy_of(kind, mask, peer, number):
        there = mask ^ peer
        return pltpu.make_async_remote_copy(
            src_ref=block_of(kind, mask),
            dst_ref=block_of(kind, there),
            send_sem=send_sem.at[number],
            recv_sem=(recv_a if kind == "a" else recv_g).at[there - 1],
            device_id={"dp": flip_bits(me, peer)},
            device_id_type=MESH,
        )

    def send(kind, mask, peer):
        copy = copy_of(kind, mask, peer, len(started))
        copy.start()
        started.append(copy)

    def arrived(kind, mask):
        copy_of(kind, 0, mask, 0).wait_recv()

    def square_columns():
        gram = jnp.dot(
            acts[...], acts_t[...].reshape(rows_all, -1), preferred_element_type=jnp.float32
        )
        high = gram.astype(jnp.bfloat16)
        rest = gram - high.astype(jnp.float32)
        middle = rest.astype(jnp.bfloat16)
        low = (rest - middle.astype(jnp.float32)).astype(jnp.bfloat16)

        @pl.loop(0, grad.shape[0])
        def _(tile):
            piece = grad[tile]
            product = jnp.dot(low, piece, preferred_element_type=jnp.float32)
            product += jnp.dot(middle, piece, preferred_element_type=jnp.float32)
            product += jnp.dot(high, piece, preferred_element_type=jnp.float32)
            squares[0, tile] = jnp.sum(
                piece.astype(jnp.float32) * product, axis=0, keepdims=True
            )

    def square_copy(mask):
        return pltpu.make_async_remote_copy(
            src_ref=squares.at[0],
            dst_ref=squares.at[mask],
            send_sem=send_q.at[mask - 1],
            recv_sem=recv_q.at[mask - 1],
            device_id={"dp": flip_bits(me, mask)},
            device_id_type=MESH,
        )

    def add_blocks(masks, first, last):
        def product(mask, block, tile):
            return jnp.dot(
                held_a[mask][block], held_g[mask][tile], preferred_element_type=jnp.float32
            )

        @pl.loop(0, capacity)
        def _(slot):
            block, tile = block_slot[slot], tile_slot[slot]
            value = None if first else total[slot]
            for mask in masks:
                part = product(mask, block, tile)
                part = part.astype(jnp.bfloat16).astype(jnp.float32)
                value = part if value is None else value + part
            if last:
                offload[slot] = value.astype(jnp.bfloat16)
            else:
                total[slot] = value

        for i in range(sel_count):
            tile = sel_tile[i]
            place = pl.ds(i * TILE, TILE)
            value = None if first else sel_sum[:, place]
            for mask in masks:
                part = product(mask, me, tile)
                value = part if value is None else value + part
            sel_sum[:, place] = value

    if n == 8:
        core, near, far = 1, 2, 4
        send("g", 0, near)
        send("a", 0, far)
        send("a", 0, core)
        send("g", 0, core)
        send("a", 0, near)
        send("g", 0, far)
        square_columns()
        arrived("a", core)
        arrived("g", core)
        add_blocks((0, core), True, False)
        for mask in range(1, n):
            square_copy(mask).start()
        arrived("g", near)
        send("g", near, far)
        send("g", near, core)
        arrived("a", far)
        send("a", far, near)
        send("a", far, core)
        arrived("a", near)
        send("a", near, core)
        arrived("g", far)
        send("g", far, core)
        for mask in (near, far):
            arrived("a", mask ^ core)
            arrived("g", mask ^ core)
        add_blocks((near, near ^ core, far, far ^ core), False, False)
        both = near ^ far
        arrived("a", both)
        send("a", both, core)
        arrived("g", both)
        send("g", both, core)
        arrived("a", both ^ core)
        arrived("g", both ^ core)
        add_blocks((both, both ^ core), False, True)
    else:
        for mask in range(1, n):
            send("g", 0, mask)
            send("a", 0, mask)
        square_columns()
        add_blocks((0,), True, False)
        for mask in range(1, n):
            square_copy(mask).start()
        for mask in range(1, n):
            arrived("a", mask)
            arrived("g", mask)
            add_blocks((mask,), False, mask == n - 1)

    whole = squares[0]
    for mask in range(1, n):
        square_copy(mask).wait_recv()
        whole = whole + squares[mask]
    norm[...] = jnp.sqrt(whole)
    for copy in started:
        copy.wait_send()
    for mask in range(1, n):
        square_copy(mask).wait_send()


def body(
    acts,
    grad_out,
    selected,
    owner,
    sel_weight,
    sel_moment,
    sel_second,
    off_weight,
    off_moment,
    off_second,
):
    n = lax.axis_size("dp")
    tokens_here, rows_all = acts.shape
    cols_here = grad_out.shape[1]
    tiles_here = cols_here // TILE
    sel_count = selected.shape[1]
    rest_count = tiles_here - sel_count
    row_block = rows_all // n
    capacity = off_weight.shape[2]
    piece_count = rest_count * n
    selected_row = selected[0]
    owner_row = owner[0, :, 0]
    mine = (owner_row == lax.axis_index("dp")).astype(jnp.int32)
    pieces = jnp.arange(piece_count, dtype=jnp.int32)
    before = jnp.sum(mine[None, :] * (pieces[:, None] > pieces[None, :]), axis=1)
    taken = mine[None, :] * (before[None, :] == jnp.arange(capacity)[:, None])
    piece = jnp.sum(taken * pieces[None, :], axis=1)
    filled = jnp.sum(taken, axis=1) > 0
    order = piece // n
    tiles = jnp.arange(tiles_here, dtype=jnp.int32)
    free = 1 - jnp.any(tiles[:, None] == selected_row[None, :], axis=1).astype(jnp.int32)
    rank = jnp.sum(free[None, :] * (tiles[:, None] > tiles[None, :]), axis=1)
    named = free[None, :] * (rank[None, :] == order[:, None])
    tile_slot = jnp.sum(named * tiles[None, :], axis=1).astype(jnp.int32)
    block_slot = (piece % n).astype(jnp.int32)

    acts_t = acts.T.reshape(n, row_block, tokens_here)
    grad_tiles = jnp.moveaxis(grad_out.reshape(tokens_here, tiles_here, TILE), 1, 0)
    sends = 14 if n == 8 else 2 * (n - 1)
    in_vmem = pl.BlockSpec(memory_space=pltpu.VMEM)
    in_smem = pl.BlockSpec(memory_space=pltpu.SMEM)
    offload, sel_sum, norm = pl.pallas_call(
        functools.partial(gather_kernel, n),
        out_shape=(
            jax.ShapeDtypeStruct((capacity, row_block, TILE), jnp.bfloat16),
            jax.ShapeDtypeStruct((row_block, sel_count * TILE), jnp.float32),
            jax.ShapeDtypeStruct((tiles_here, 1, TILE), jnp.float32),
        ),
        in_specs=[in_smem] * 3 + [in_vmem] * 3,
        out_specs=(in_vmem,) * 3,
        scratch_shapes=[
            pltpu.VMEM((capacity, row_block, TILE), jnp.float32),
            pltpu.VMEM((n, tiles_here, 1, TILE), jnp.float32),
            pltpu.SemaphoreType.DMA((sends,)),
            pltpu.SemaphoreType.DMA((n - 1,)),
            pltpu.SemaphoreType.DMA((n - 1,)),
            pltpu.SemaphoreType.DMA((n - 1,)),
            pltpu.SemaphoreType.DMA((n - 1,)),
        ]
        + [pltpu.VMEM((n, row_block, tokens_here), jnp.bfloat16)] * (n - 1)
        + [pltpu.VMEM((tiles_here, tokens_here, TILE), jnp.bfloat16)] * (n - 1),
        compiler_params=pltpu.CompilerParams(
            collective_id=0, has_side_effects=True, vmem_limit_bytes=VMEM_LIMIT
        ),
    )(tile_slot, block_slot, selected_row, acts, acts_t, grad_tiles)
    new_sel = adam_update(sel_weight, sel_moment, sel_second, sel_sum)
    zero_half = jnp.zeros((), jnp.bfloat16)
    off_grad = jnp.where(filled[:, None, None], offload, zero_half).astype(jnp.float32)
    new_off = adam_update(
        off_weight, off_moment, off_second, off_grad.reshape(off_weight.shape)
    )
    return (norm.reshape(cols_here), *new_sel, *new_off)


def solution(mesh):
    placed = (
        P("dp", None),
        P("dp", "tensor"),
        P("tensor", None),
        P("tensor", None, None),
        P("dp", "tensor"),
        P("dp", "tensor"),
        P("dp", "tensor"),
        P("dp", "tensor", None, None, None),
        P("dp", "tensor", None, None, None),
        P("dp", "tensor", None, None, None),
    )
    return jax.shard_map(
        body,
        mesh=mesh,
        in_specs=placed,
        out_specs=(
            P("tensor"),
            P("dp", "tensor"),
            P("dp", "tensor"),
            P("dp", "tensor"),
            P("dp", "tensor", None, None, None),
            P("dp", "tensor", None, None, None),
            P("dp", "tensor", None, None, None),
        ),
        check_vma=False,
    )
```

time: 672 us -> 123 us (0.18)
  blocking collectives: 445 us -> 0 us
  Pallas kernels: 0 us -> 87.4 us
  local copies, waits for them, and re-layouts: 82.4 us -> 5.11 us
  matrix products: 48.3 us -> 0 us
  other arithmetic: 72.8 us -> 29.2 us
  between operations: 14.2 us -> 0.73 us
  starting transfers between devices: 7.63 us -> 0 us
    psum x1 -> x0, blocking collectives: 445 us -> none  [body(): column_norm = jnp.sqrt(lax.psum(squares, 'dp'))]
    pallas_call x0 -> x1, Pallas kernels: none -> 87.4 us  [body(): pl.pallas_call(functools.partial(gather_kernel, n), out_shape=(jax.ShapeD...]
    dot_general x27 -> x0, matrix products: 48.3 us -> none  [the longest x25 45.4 us: contract_tokens(): lax.dot_general(left, right, (((0,), (0,)), ((), ())), preferred_element_...]
    dynamic_update_slice x48 -> x0, local copies, waits for them, and re-layouts: 41.3 us -> none  [body(): lax.map(tile_partial, rest_grad)]
    select_n x6 -> x1, other arithmetic: 27.4 us -> 0.53 us  [body(): block_slot = (piece % n).astype(jnp.int32)]
    gather x4 -> x0, local copies, waits for them, and re-layouts: 24.8 us -> none  [the longest x1 23.4 us: body(): flat_pieces[jnp.minimum(source, piece_count - 1)]]
    reduce_sum x2 -> x4, other arithmetic: 16.5 us -> 0.96 us  [the longest x1 0.61 us: body(): tile_slot = jnp.sum(named * tiles[None, :], axis=1).astype(jnp.int32)]
    unnamed x11, local copies, waits for them, and re-layouts: 13.6 us -> 1.58 us
  transfers between devices with their start and end apart: 2 -> 0, of which waited for: 0 -> 0; matrix products, arithmetic and copies ran while one was open for 4% -> 0% of each run, Pallas kernels for 0% -> 0%
where the time goes in v1:
time: 123 us; the launch traced here: 122 us
  Pallas kernels  87.4 us (71%)
  other arithmetic  29.2 us (24%)
  local copies, waits for them, and re-layouts  5.11 us (4%)
    pallas_call x1, Pallas kernels, body(): pl.pallas_call(functools.partial(gather_kernel, n), out_shape=(jax.ShapeD...  87.4 us
    sub x2, other arithmetic, adam_update(): weight - learn_rate * (update + decay_rate * weight)  25.6 us

profile of v1, /device:TPU:0, one launch (start us, length us, event | category | flops | bytes accessed | tf_op | source)
XLA Modules:
  0.0 122.4 jit_solution(14860934263039563268)
XLA Ops:
  0.6 0.7 compare_convert_fusion
  1.3 0.1 select_reduce_fusion
  1.4 0.1 select_reduce_fusion.1
  1.6 0.5 and_select_fusion
  2.1 0.7 fusion.6
  2.8 0.1 select_reduce_fusion.2
  3.0 0.6 multiply_reduce_fusion.tile_slot
  3.6 1.5 %copy.22 = bf16[128,3584]{0,1:T(8,128)(2,1)S(1)} copy(bf16[128,3584]{1,0:T(8,128)(2,1)} %param.11) | data formatting | bytes 1835008 | tf_op args[1]
  5.1 1.3 %copy.23 = bf16[128,28,128]{2,0,1:T(8,128)(2,1)} copy(bf16[128,28,128]{0,2,1:T(8,128)(2,1)S(1)} %bitcast.19) | data formatting | bytes 1835008 | tf_op jit(solution)/shard_map/reshape | solution.py:255
  6.4 2.3 %copy.21 = bf16[4096,128]{1,0:T(8,128)(2,1)} copy(bf16[4096,128]{0,1:T(8,128)(2,1)} %bitcast.17) | data formatting | bytes 2097152 | tf_op jit(solution)/shard_map/transpose | solution.py:254
  8.7 87.4 %shard_map.153 = (bf16[36,512,128]{2,1,0:T(8,128)(2,1)}, f32[512,512]{1,0:T(8,128)}, f32[28,1,128]{2,1,0:T(1,128)}) custom-call(s32[36]{0:T(128)} %multiply_reduce_fusion.tile_slot, s32[36]{0:T(128)} %get-tuple-element.21.block_slot, s32[4]{0:T(128)} %bitcast.25, bf16[128,4096]{1,0:T(8,128)(2,1)} %acts.1, bf16[8,512,128]{2,1,0:T(8,128)(2,1)} %bitcast.18, ...), custom_call_target="tpu_custom_call" | custom-call | tf_op jit(solution)/shard_map/pallas_call | solution.py:259
  96.1 0.0 copy-start
  96.1 0.0 copy-start.1
  96.1 0.0 copy-start.2
  96.1 0.0 copy-start.3
  96.1 0.0 copy-start.4
  96.1 23.4 %multiply_subtract_fusion = (f32[1,1,36,512,128]{4,3,2,1,0:T(8,128)}, f32[1,1,36,512,128]{4,3,2,1,0:T(8,128)}, f32[1,1,36,512,128]{4,3,2,1,0:T(8,128)}) fusion(f32[1,1,36,512,128]{4,3,2,1,0:T(8,128)} %param.17, bf16[36,512,128]{2,1,0:T(8,128)(2,1)} %get-tuple-element.12, pred[36]{0:T(512)(128)(4,1)S(1)} %broadcast_compare_fusion, ...), kind=kLoop, calls=%fused_computation.6 | loop fusion | flops 40108032 | bytes 61341732 | tf_op jit(solution)/shard_map/sub | solution.py:28
  119.5 0.0 copy-done
  119.5 0.0 copy-done.1
  119.5 0.0 copy-done.2
  119.5 0.0 copy-done.3
  119.5 2.3 %multiply_subtract_fusion.1 = (f32[512,512]{1,0:T(8,128)}, f32[512,512]{1,0:T(8,128)}, f32[512,512]{1,0:T(8,128)}) fusion(f32[512,512]{1,0:T(8,128)S(1)} %copy-done, f32[512,512]{1,0:T(8,128)S(1)} %copy-done.3, f32[512,512]{1,0:T(8,128)S(1)} %copy-done.1, f32[512,512]{1,0:T(8,128)S(1)} %copy-done.2), kind=kLoop, calls=%fused_computation.10 | loop fusion | flops 3932160 | bytes 7340032 | tf_op jit(solution)/shard_map/sub | solution.py:28
  121.8 0.0 copy-done.4
  121.8 0.6 reduce
  (2 shorter events, 0.0 us)
Async XLA Ops:
  96.1 23.4 %copy-start = (f32[512,512]{1,0:T(8,128)S(1)}, f32[512,512]{1,0:T(8,128)}, u32[]{:S(2)}) copy-start(f32[512,512]{1,0:T(8,128)} %param.14) | copy-start | bytes 3145732
  96.1 23.4 %copy-start.1 = (f32[512,512]{1,0:T(8,128)S(1)}, f32[512,512]{1,0:T(8,128)}, u32[]{:S(2)}) copy-start(f32[512,512]{1,0:T(8,128)} %param.15) | copy-start | bytes 3145732
  96.1 23.4 %copy-start.2 = (f32[512,512]{1,0:T(8,128)S(1)}, f32[512,512]{1,0:T(8,128)}, u32[]{:S(2)}) copy-start(f32[512,512]{1,0:T(8,128)} %param.16) | copy-start | bytes 3145732
  96.1 23.4 %copy-start.3 = (f32[512,512]{1,0:T(8,128)S(1)}, f32[512,512]{1,0:T(8,128)}, u32[]{:S(2)}) copy-start(f32[512,512]{1,0:T(8,128)} %get-tuple-element.11) | copy-start | bytes 3145732
  96.1 25.7 %copy-start.4 = (f32[28,1,128]{2,1,0:T(1,128)S(1)}, f32[28,1,128]{2,1,0:T(1,128)}, u32[]{:S(2)}) copy-start(f32[28,1,128]{2,1,0:T(1,128)} %get-tuple-element.10) | copy-start | bytes 43012

commit v2 on v1

--- a/solution.py
+++ b/solution.py
@@ -42,6 +42,7 @@
 
 def gather_kernel(
     n,
+    paired,
     tile_slot,
     block_slot,
     sel_tile,
@@ -55,12 +56,23 @@
     squares,
     send_sem,
     recv_a,
+    recv_z,
     recv_g,
+    recv_e,
     send_q,
     recv_q,
     *held,
 ):
     held_a, held_g = (acts_t,) + held[: n - 1], (grad,) + held[n - 1 :]
+    layer = lax.axis_index("tensor")
+    half, cut = n // 2, grad.shape[0] * 3 // 4
+    side = layer % 2
+    parts = {
+        "a": (held_a, pl.ds(side * half, half), recv_a),
+        "z": (held_a, pl.ds((1 - side) * half, half), recv_z),
+        "g": (held_g, pl.ds(0, cut), recv_g),
+        "e": (held_g, pl.ds(cut, grad.shape[0] - cut), recv_e),
+    }
     me = lax.axis_index("dp")
     capacity = offload.shape[0]
     sel_count = sel_tile.shape[0]
@@ -71,23 +83,41 @@
         pl.semaphore_signal(
             barrier, inc=1, device_id={"dp": flip_bits(me, mask)}, device_id_type=MESH
         )
-    pl.semaphore_wait(barrier, n - 1)
+    if paired:
+        pl.semaphore_signal(
+            barrier, inc=1, device_id={"tensor": flip_bits(layer, 1)}, device_id_type=MESH
+        )
+    pl.semaphore_wait(barrier, n if paired else n - 1)
 
     started = []
 
-    def block_of(kind, mask):
-        return (held_a if kind == "a" else held_g)[mask]
+    def part_of(kind, mask):
+        slots, place, _ = parts[kind]
+        return slots[mask].at[place]
 
     def copy_of(kind, mask, peer, number):
         there = mask ^ peer
         return pltpu.make_async_remote_copy(
-            src_ref=block_of(kind, mask),
-            dst_ref=block_of(kind, there),
+            src_ref=part_of(kind, mask),
+            dst_ref=part_of(kind, there),
             send_sem=send_sem.at[number],
-            recv_sem=(recv_a if kind == "a" else recv_g).at[there - 1],
+            recv_sem=parts[kind][2].at[there - 1],
             device_id={"dp": flip_bits(me, peer)},
             device_id_type=MESH,
         )
+
+    def send_across(mask):
+        part = part_of("a", mask)
+        copy = pltpu.make_async_remote_copy(
+            src_ref=part,
+            dst_ref=part,
+            send_sem=send_sem.at[len(started)],
+            recv_sem=recv_z.at[mask - 1],
+            device_id={"tensor": flip_bits(layer, 1)},
+            device_id_type=MESH,
+        )
+        copy.start()
+        started.append(copy)
 
     def send(kind, mask, peer):
         copy = copy_of(kind, mask, peer, len(started))
@@ -154,53 +184,71 @@
                 value = part if value is None else value + part
             sel_sum[:, place] = value
 
-    if n == 8:
-        core, near, far = 1, 2, 4
-        send("g", 0, near)
-        send("a", 0, far)
-        send("a", 0, core)
-        send("g", 0, core)
-        send("a", 0, near)
-        send("g", 0, far)
-        square_columns()
-        arrived("a", core)
-        arrived("g", core)
-        add_blocks((0, core), True, False)
+    def relay(kinds, mask):
+        for kind in kinds:
+            arrived(kind, mask)
+            send(kind, mask, 1)
+
+    def complete(mask):
+        for kind in parts:
+            arrived(kind, mask)
+
+    def send_squares():
         for mask in range(1, n):
             square_copy(mask).start()
+
+    if paired:
+        core, near, far = 1, 2, 4
+        both = near ^ far
+        send("a", 0, near)
+        send("a", 0, far)
+        send("g", 0, near)
+        send("g", 0, far)
+        send("e", 0, far)
+        for kind in parts:
+            send(kind, 0, core)
+        square_columns()
+        arrived("a", far)
+        send("a", far, near)
+        send("e", 0, near)
+        send_across(far)
+        send("a", far, core)
+        arrived("a", near)
+        send_across(near)
+        send("a", near, core)
+        complete(core)
+        add_blocks((0, core), True, False)
+        send_squares()
+        relay("z", far)
         arrived("g", near)
         send("g", near, far)
         send("g", near, core)
-        arrived("a", far)
-        send("a", far, near)
-        send("a", far, core)
-        arrived("a", near)
-        send("a", near, core)
-        arrived("g", far)
-        send("g", far, core)
-        for mask in (near, far):
-            arrived("a", mask ^ core)
-            arrived("g", mask ^ core)
-        add_blocks((near, near ^ core, far, far ^ core), False, False)
-        both = near ^ far
+        arrived("e", far)
+        send("e", far, near)
+        send("e", far, core)
+        relay("g", far)
+        add_blocks((far,), False, False)
         arrived("a", both)
+        send_across(both)
         send("a", both, core)
-        arrived("g", both)
-        send("g", both, core)
-        arrived("a", both ^ core)
-        arrived("g", both ^ core)
+        relay("z", near)
+        complete(far ^ core)
+        add_blocks((far ^ core,), False, False)
+        relay("e", near)
+        complete(near ^ core)
+        add_blocks((near, near ^ core), False, False)
+        relay("gez", both)
+        complete(both ^ core)
         add_blocks((both, both ^ core), False, True)
     else:
         for mask in range(1, n):
-            send("g", 0, mask)
-            send("a", 0, mask)
+            for kind in parts:
+                send(kind, 0, mask)
         square_columns()
         add_blocks((0,), True, False)
+        send_squares()
         for mask in range(1, n):
-            square_copy(mask).start()
-        for mask in range(1, n):
-            arrived("a", mask)
-            arrived("g", mask)
+            complete(mask)
             add_blocks((mask,), False, mask == n - 1)
 
     whole = squares[0]
@@ -253,11 +301,12 @@
 
     acts_t = acts.T.reshape(n, row_block, tokens_here)
     grad_tiles = jnp.moveaxis(grad_out.reshape(tokens_here, tiles_here, TILE), 1, 0)
-    sends = 14 if n == 8 else 2 * (n - 1)
+    paired = n == 8 and lax.axis_size("tensor") % 2 == 0
+    sends = 28 if paired else 4 * (n - 1)
     in_vmem = pl.BlockSpec(memory_space=pltpu.VMEM)
     in_smem = pl.BlockSpec(memory_space=pltpu.SMEM)
     offload, sel_sum, norm = pl.pallas_call(
-        functools.partial(gather_kernel, n),
+        functools.partial(gather_kernel, n, paired),
         out_shape=(
             jax.ShapeDtypeStruct((capacity, row_block, TILE), jnp.bfloat16),
             jax.ShapeDtypeStruct((row_block, sel_count * TILE), jnp.float32),
@@ -269,6 +318,8 @@
             pltpu.VMEM((capacity, row_block, TILE), jnp.float32),
             pltpu.VMEM((n, tiles_here, 1, TILE), jnp.float32),
             pltpu.SemaphoreType.DMA((sends,)),
+            pltpu.SemaphoreType.DMA((n - 1,)),
+            pltpu.SemaphoreType.DMA((n - 1,)),
             pltpu.SemaphoreType.DMA((n - 1,)),
             pltpu.SemaphoreType.DMA((n - 1,)),
             pltpu.SemaphoreType.DMA((n - 1,)),

time: 123 us -> 111 us (0.902)
  Pallas kernels: 87.4 us -> 76.1 us
    pallas_call x1, Pallas kernels: 87.4 us -> 76.1 us  [body(): pl.pallas_call(functools.partial(gather_kernel, n, paired), out_shape=(ja...]
where the time goes in v2:
time: 111 us
  Pallas kernels  76.1 us (69%)
  other arithmetic  29.2 us (26%)
  local copies, waits for them, and re-layouts  5.11 us (5%)
    pallas_call x1, Pallas kernels, body(): pl.pallas_call(functools.partial(gather_kernel, n, paired), out_shape=(ja...  76.1 us
    sub x2, other arithmetic, adam_update(): weight - learn_rate * (update + decay_rate * weight)  25.6 us
    transpose x1, local copies, waits for them, and re-layouts, body(): acts_t = acts.T.reshape(n, row_block, tokens_here)  2.26 us

profile of v2, /device:TPU:0, one launch (start us, length us, event | category | flops | bytes accessed | tf_op | source)
XLA Modules:
  0.0 111.1 jit_solution(9246458055383846923)
XLA Ops:
  0.6 0.7 compare_convert_fusion
  1.3 0.1 select_reduce_fusion
  1.4 0.1 select_reduce_fusion.1
  1.6 0.5 and_select_fusion
  2.1 0.7 fusion.6
  2.8 0.1 select_reduce_fusion.2
  3.0 0.6 multiply_reduce_fusion.tile_slot
  3.6 1.5 %copy.22 = bf16[128,3584]{0,1:T(8,128)(2,1)S(1)} copy(bf16[128,3584]{1,0:T(8,128)(2,1)} %param.11) | data formatting | bytes 1835008 | tf_op args[1]
  5.1 1.3 %copy.23 = bf16[128,28,128]{2,0,1:T(8,128)(2,1)} copy(bf16[128,28,128]{0,2,1:T(8,128)(2,1)S(1)} %bitcast.19) | data formatting | bytes 1835008 | tf_op jit(solution)/shard_map/reshape | solution.py:303
  6.4 2.3 %copy.21 = bf16[4096,128]{1,0:T(8,128)(2,1)} copy(bf16[4096,128]{0,1:T(8,128)(2,1)} %bitcast.17) | data formatting | bytes 2097152 | tf_op jit(solution)/shard_map/transpose | solution.py:302
  8.7 76.1 %shard_map.153 = (bf16[36,512,128]{2,1,0:T(8,128)(2,1)}, f32[512,512]{1,0:T(8,128)}, f32[28,1,128]{2,1,0:T(1,128)}) custom-call(s32[36]{0:T(128)} %multiply_reduce_fusion.tile_slot, s32[36]{0:T(128)} %get-tuple-element.21.block_slot, s32[4]{0:T(128)} %bitcast.25, bf16[128,4096]{1,0:T(8,128)(2,1)} %acts.1, bf16[8,512,128]{2,1,0:T(8,128)(2,1)} %bitcast.18, ...), custom_call_target="tpu_custom_call" | custom-call | tf_op jit(solution)/shard_map/pallas_call | solution.py:308
  84.8 0.0 copy-start
  84.8 0.0 copy-start.1
  84.8 0.0 copy-start.2
  84.8 0.0 copy-start.3
  84.8 0.0 copy-start.4
  84.8 23.4 %multiply_subtract_fusion = (f32[1,1,36,512,128]{4,3,2,1,0:T(8,128)}, f32[1,1,36,512,128]{4,3,2,1,0:T(8,128)}, f32[1,1,36,512,128]{4,3,2,1,0:T(8,128)}) fusion(f32[1,1,36,512,128]{4,3,2,1,0:T(8,128)} %param.17, bf16[36,512,128]{2,1,0:T(8,128)(2,1)} %get-tuple-element.12, pred[36]{0:T(512)(128)(4,1)S(1)} %broadcast_compare_fusion, ...), kind=kLoop, calls=%fused_computation.6 | loop fusion | flops 40108032 | bytes 61341732 | tf_op jit(solution)/shard_map/sub | solution.py:28
  108.2 0.0 copy-done
  108.2 0.0 copy-done.1
  108.2 0.0 copy-done.2
  108.2 0.0 copy-done.3
  108.2 2.3 %multiply_subtract_fusion.1 = (f32[512,512]{1,0:T(8,128)}, f32[512,512]{1,0:T(8,128)}, f32[512,512]{1,0:T(8,128)}) fusion(f32[512,512]{1,0:T(8,128)S(1)} %copy-done, f32[512,512]{1,0:T(8,128)S(1)} %copy-done.3, f32[512,512]{1,0:T(8,128)S(1)} %copy-done.1, f32[512,512]{1,0:T(8,128)S(1)} %copy-done.2), kind=kLoop, calls=%fused_computation.10 | loop fusion | flops 3932160 | bytes 7340032 | tf_op jit(solution)/shard_map/sub | solution.py:28
  110.5 0.0 copy-done.4
  110.5 0.6 reduce
  (2 shorter events, 0.0 us)
Async XLA Ops:
  84.8 23.4 %copy-start = (f32[512,512]{1,0:T(8,128)S(1)}, f32[512,512]{1,0:T(8,128)}, u32[]{:S(2)}) copy-start(f32[512,512]{1,0:T(8,128)} %param.14) | copy-start | bytes 3145732
  84.8 23.4 %copy-start.1 = (f32[512,512]{1,0:T(8,128)S(1)}, f32[512,512]{1,0:T(8,128)}, u32[]{:S(2)}) copy-start(f32[512,512]{1,0:T(8,128)} %param.15) | copy-start | bytes 3145732
  84.8 23.4 %copy-start.2 = (f32[512,512]{1,0:T(8,128)S(1)}, f32[512,512]{1,0:T(8,128)}, u32[]{:S(2)}) copy-start(f32[512,512]{1,0:T(8,128)} %param.16) | copy-start | bytes 3145732
  84.8 23.4 %copy-start.3 = (f32[512,512]{1,0:T(8,128)S(1)}, f32[512,512]{1,0:T(8,128)}, u32[]{:S(2)}) copy-start(f32[512,512]{1,0:T(8,128)} %get-tuple-element.11) | copy-start | bytes 3145732
  84.8 25.7 %copy-start.4 = (f32[28,1,128]{2,1,0:T(1,128)S(1)}, f32[28,1,128]{2,1,0:T(1,128)}, u32[]{:S(2)}) copy-start(f32[28,1,128]{2,1,0:T(1,128)} %get-tuple-element.10) | copy-start | bytes 43012
